TPU v7x, 32 devices: a whole 2x2x4 slice. The times are simulated.
32 devices in a mesh: row: 4 (over y, x), col: 8 (over z, core).
Axes of the slice: x: 2, y: 2, z: 4, core: 2. Of those that a mesh axis runs over, the one named last changes fastest.
Arguments:
- activations: bfloat16 [1024, 9216], P('col', 'row'), may hold values from -64 to 64
- output_grads: bfloat16 [1024, 73728], P('row', 'col'), may hold values from -16 to 16
- weight: bfloat16 [9216, 73728], P('row', 'col'), may hold values from -1 to 1
- row_moment: float32 [9216], P('row'), may hold values from 0.01 to 0.3
- col_moment: float32 [73728], P('col'), may hold values from 0.01 to 0.3
Outputs:
- new_weight: bfloat16 [9216, 73728], P('row', 'col')
- new_row: float32 [9216], P('row')
- new_col: float32 [73728], P('col')
All inputs are finite; a program needn't handle non-finite values.
Results may differ from a plain program's by a relative error of at most 0.0004.
Values may be sent and summed in bfloat16 or wider, within the bound.
No kernel may reach another device: no remote copies, remote signals or barrier semaphores. Data moves between devices by JAX's collectives and lax.ppermute only.
A program may use at most 256 MiB of HBM per device.

v0:
```python
import jax
import jax.numpy as jnp
from jax import lax
from jax.sharding import PartitionSpec as P

ADDED_SQUARE = 1e-30
DECAY_RATE = 0.8
CLIP_LIMIT = 1.0
STEP_SIZE = 0.1
MEAN_OFFSET = 1e-06


def on_device(activations, output_grads, weight, row_moment, col_moment):
    tile_rows, tile_cols = weight.shape
    total_rows = tile_rows * lax.axis_size("row")
    total_cols = tile_cols * lax.axis_size("col")
    entries = float(total_rows * total_cols)
    weight_wide = weight.astype(jnp.float32)
    weight_local = jnp.sum(weight_wide * weight_wide)
    weight_total = lax.psum(weight_local, ("row", "col"))
    contract = (((0,), (0,)), ((), ()))
    acts_all = lax.all_gather(activations, "col", axis=0, tiled=True)
    gradient = lax.dot_general(
        acts_all,
        lax.all_gather(output_grads, "row", axis=0, tiled=True),
        contract,
        preferred_element_type=jnp.float32,
    )
    squared = gradient * gradient
    row_part = jnp.sum(squared + ADDED_SQUARE, axis=1)
    col_part = jnp.sum(squared + ADDED_SQUARE, axis=0)
    row_total = lax.psum(row_part, "col")
    col_total = lax.psum(col_part, "row")
    new_row = DECAY_RATE * row_moment + (1.0 - DECAY_RATE) * row_total / total_cols
    new_col = DECAY_RATE * col_moment + (1.0 - DECAY_RATE) * col_total / total_rows
    inverse = lax.rsqrt(new_row[:, None] * new_col[None, :])
    ratio_local = jnp.sum(squared * inverse * inverse)
    leader = (lax.axis_index("col") == 0).astype(jnp.float32)
    row_local = leader * jnp.sum(new_row)
    row_sum, ratio_sum = lax.psum((row_local, ratio_local), ("row", "col"))
    row_mean = row_sum / total_rows
    rms_update = jnp.sqrt(row_mean * ratio_sum / entries)
    clip_factor = jnp.maximum(1.0, rms_update / CLIP_LIMIT)
    step_scale = STEP_SIZE * jnp.sqrt(weight_total / entries + MEAN_OFFSET)
    update = gradient * inverse * jnp.sqrt(row_mean)
    new_weight = (weight_wide - step_scale / clip_factor * update).astype(jnp.bfloat16)
    return (new_weight, new_row, new_col)


def solution(mesh):
    return jax.shard_map(
        on_device,
        mesh=mesh,
        in_specs=(P("col", "row"), P("row", "col"), P("row", "col"), P("row"), P("col")),
        out_specs=(P("row", "col"), P("row"), P("col")),
        check_vma=False,
    )
```

profile of v0, /device:TPU:12, one launch (start us, length us, event | category | flops | bytes accessed | tf_op | source)
XLA Modules:
  0.0 471.2 jit_solution(5277439258976595096)
XLA Ops:
  7.2 0.0 all-gather.3.cloned.1.call-start
  7.2 0.7 all-gather.3.cloned.1.call-update
  7.9 0.0 all-gather.5.cloned.1.call-start
  7.9 0.7 all-gather.5.cloned.1.call-update
  8.7 24.5 %fusion = f32[]{:T(128)} fusion(bf16[2304,9216]{1,0:T(8,128)(2,1)} %param.7), kind=kLoop, calls=%fused_computation.3 | loop fusion | flops 63700992 | bytes 42467332 | tf_op jit(solution)/shard_map/reduce_sum | solution.py:19
  33.1 0.0 copy-start.2
  33.2 0.0 copy-start.3
  33.2 27.4 %all-gather.3.cloned.1.call-done = bf16[1024,2304]{1,0:T(8,128)(2,1)} async-done(((bf16[128,2304]{1,0:T(8,128)(2,1)}), bf16[1024,2304]{1,0:T(8,128)(2,1)}) %all-gather.3.cloned.1.call-update) | async-done | bytes 4718608 | tf_op jit(solution)/shard_map/all_gather | solution.py:22
  60.5 177.9 %all-gather.5.cloned.1.call-done = bf16[1024,9216]{1,0:T(8,128)(2,1)} async-done(((bf16[256,9216]{1,0:T(8,128)(2,1)}), bf16[1024,9216]{1,0:T(8,128)(2,1)}) %all-gather.5.cloned.1.call-update) | async-done | bytes 18874384 | tf_op jit(solution)/shard_map/all_gather | solution.py:25
  238.4 59.5 %add_reduce_fusion = (f32[9216]{0:T(1024)S(1)}, f32[2304]{0:T(1024)S(1)}, f32[2304,9216]{1,0:T(8,128)}) fusion(bf16[1024,2304]{1,0:T(8,128)(2,1)} %all-gather.3.cloned.1.call-done, bf16[1024,9216]{1,0:T(8,128)(2,1)} %all-gather.5.cloned.1.call-done), kind=kOutput, calls=%fused_computation.7 | convolution fusion | flops 43571466240 | bytes 108573696 | tf_op jit(solution)/shard_map/dot_general | solution.py:23
  297.9 15.7 %psum.38 = f32[9216]{0:T(1024)S(1)} all-reduce(f32[9216]{0:T(1024)S(1)} %get-tuple-element.3), channel_id=1, replica_groups=mesh['row'=4,'col'=8] {'row'}, use_global_device_ids=true, to_apply=%region_7.0 | all-reduce | flops 9216 | bytes 73728 | tf_op jit(solution)/shard_map/psum | solution.py:33
  313.6 22.4 %psum.36 = f32[2304]{0:T(1024)S(1)} all-reduce(f32[2304]{0:T(1024)S(1)} %get-tuple-element.4), channel_id=1, replica_groups=mesh['row'=4,'col'=8] {'col'}, use_global_device_ids=true, to_apply=%region_3.0 | all-reduce | flops 2304 | bytes 18432 | tf_op jit(solution)/shard_map/psum | solution.py:32
  336.0 0.0 copy-done.2
  336.0 0.0 copy-done.3
  336.0 0.0 copy-start
  336.0 0.6 fusion.3
  336.6 0.0 copy-start.1
  336.6 28.1 %fusion.2 = f32[]{:T(128)} fusion(f32[2304,9216]{1,0:T(8,128)} %get-tuple-element.10, f32[9216]{0:T(1024)S(1)} %multiply_add_fusion, f32[2304]{0:T(1024)S(1)} %get-tuple-element.9), kind=kLoop, calls=%fused_computation.5 | loop fusion | flops 106168320 | bytes 84980736 | tf_op jit(solution)/shard_map/reduce_sum | solution.py:37
  365.4 43.2 %all-reduce = (f32[]{:T(128)}, f32[]{:T(128)}, f32[]{:T(128)}) all-reduce(f32[]{:T(128)S(6)} %mul.66, f32[]{:T(128)} %fusion, f32[]{:T(128)} %fusion.2), channel_id=1, replica_groups=mesh['row'=4,'col'=8] {'row','col'}, use_global_device_ids=true, to_apply=%region_5.0 | all-reduce | flops 3 | bytes 24 | tf_op jit(solution)/shard_map/psum | solution.py:40
  410.6 53.7 %fusion.1 = bf16[2304,9216]{1,0:T(8,128)(2,1)} fusion(bf16[2304,9216]{1,0:T(8,128)(2,1)} %param.7, f32[2304,9216]{1,0:T(8,128)} %get-tuple-element.10, f32[]{:T(128)S(6)} %sqrt.11, f32[]{:T(128)S(6)} %div.32, f32[9216]{0:T(1024)S(1)} %multiply_add_fusion, f32[2304]{0:T(1024)S(1)} %get-tuple-element.9), kind=kLoop, calls=%fused_computation.4 | loop fusion | flops 148635648 | bytes 169915392 | tf_op jit(solution)/shard_map/convert_element_type | solution.py:46
  464.3 0.0 copy-done
  464.3 0.0 copy-done.1
  (1 shorter events, 0.0 us)
Async XLA Ops:
  7.2 53.4 %all-gather.3.cloned.1.call-start = ((), (), s32[]{:S(2)}) async-start(), calls=%async_computation | async-start | bytes 5308416 | tf_op jit(solution)/shard_map/all_gather | solution.py:22
  7.9 230.5 %all-gather.5.cloned.1.call-start = ((), (), s32[]{:S(2)}) async-start(), calls=%async_computation.1 | async-start | bytes 23592960 | tf_op jit(solution)/shard_map/all_gather | solution.py:25
  33.1 302.8 %copy-start.2 = (f32[9216]{0:T(1024)S(1)}, f32[9216]{0:T(1024)}, u32[]{:S(2)}) copy-start(f32[9216]{0:T(1024)} %param.9) | copy-start | bytes 110596
  33.2 302.9 %copy-start.3 = (f32[2304]{0:T(1024)S(1)}, f32[2304]{0:T(1024)}, u32[]{:S(2)}) copy-start(f32[2304]{0:T(1024)} %param.8) | copy-start | bytes 27652
  336.0 128.3 %copy-start = (f32[9216]{0:T(1024)}, f32[9216]{0:T(1024)S(1)}, u32[]{:S(2)}) copy-start(f32[9216]{0:T(1024)S(1)} %multiply_add_fusion) | copy-start | bytes 110596
  336.6 127.7 %copy-start.1 = (f32[2304]{0:T(1024)}, f32[2304]{0:T(1024)S(1)}, u32[]{:S(2)}) copy-start(f32[2304]{0:T(1024)S(1)} %get-tuple-element.9) | copy-start | bytes 27652
Sparse Core Ops, SparseCore 0:
  9.6 50.8 all-gather.2
  62.4 175.9 all-gather.4
where the time goes:
time: 472 us; the launch traced here: 471 us
  waiting for transfers between devices  207 us (44%)
  other arithmetic  107 us (23%)
  blocking collectives  81.3 us (17%)
  matrix products  59.5 us (13%)
  between operations  16.8 us (4%)
    all_gather x1, waiting for transfers between devices, on_device(): lax.all_gather(output_grads, 'row', axis=0, tiled=True)  178 us
    dot_general x1, matrix products, on_device(): lax.dot_general(acts_all, lax.all_gather(output_grads, 'row', axis=0, til...  59.5 us
    convert_element_type x1, other arithmetic, on_device(): (weight_wide - step_scale / clip_factor * update).astype(jnp.bfloat16)  53.7 us
    psum x1, blocking collectives, on_device(): row_sum, ratio_sum = lax.psum((row_local, ratio_local), ('row', 'col'))  43.2 us
    reduce_sum x1, other arithmetic, on_device(): ratio_local = jnp.sum(squared * inverse * inverse)  28.1 us
    all_gather x1, waiting for transfers between devices, on_device(): acts_all = lax.all_gather(activations, 'col', axis=0, tiled=True)  27.4 us
    reduce_sum x1, other arithmetic, on_device(): weight_local = jnp.sum(weight_wide * weight_wide)  24.5 us
    psum x1, blocking collectives, on_device(): row_total = lax.psum(row_part, 'col')  22.4 us
  transfers between devices with their start and end apart: 2, of which 2 were waited for; matrix products, arithmetic and copies ran while one was open for 5% of the time, Pallas kernels for 0%

commit v1 on v0

v1 whole, which is shorter than its diff:
```python
import functools

import jax
import jax.numpy as jnp
from jax import lax
from jax.experimental import pallas as pl
from jax.experimental.pallas import tpu as pltpu
from jax.sharding import PartitionSpec as P

ADDED_SQUARE = 1e-30
DECAY_RATE = 0.8
CLIP_LIMIT = 1.0
STEP_SIZE = 0.1
MEAN_OFFSET = 1e-06
SHARES = (1, 2, 3, 3)


def swap(value, axis, stride):
    size = lax.axis_size(axis)
    return lax.ppermute(value, axis, [(i, i ^ stride) for i in range(size)])


def sum_over(value, axis):
    size = lax.axis_size(axis)
    if size & (size - 1):
        return lax.psum(value, axis)
    stride = 1
    while stride < size:
        if stride * 2 < size:
            near = swap(value, axis, stride)
            far = swap(value, axis, stride * 2)
            both = swap(value, axis, stride * 3)
            value = (value + near) + (far + both)
            stride *= 4
        else:
            value = value + swap(value, axis, stride)
            stride *= 2
    return value


def gather_over(block, axis):
    size = lax.axis_size(axis)
    if size & (size - 1):
        return lax.all_gather(block, axis, axis=0, tiled=True)
    index = lax.axis_index(axis)
    held, depth, stride = block, 0, size // 2
    while stride:
        other = swap(held, axis, stride)
        upper = (index & stride) != 0
        held = jnp.stack([jnp.where(upper, other, held), jnp.where(upper, held, other)], axis=depth)
        depth += 1
        stride //= 2
    return held.reshape((size * block.shape[0],) + block.shape[1:])


def column_cuts(width):
    unit = width // sum(SHARES)
    if unit * sum(SHARES) != width or unit % 128:
        return [(0, width)]
    cuts, start = [], 0
    for share in SHARES:
        cuts.append((start, start + share * unit))
        start += share * unit
    return cuts


def divisor_of(choices, *lengths):
    for choice in choices:
        if all(length % choice == 0 for length in lengths):
            return choice
    return None


def gradient_kernel(tile, left, right, *refs):
    grad, col_sums, row_sums = refs[-3:]
    lanes = row_sums.shape[1]

    @pl.when(pl.program_id(0) == 0)
    def _():
        row_sums[...] = jnp.zeros_like(row_sums)

    col_sums[...] = jnp.zeros_like(col_sums)

    def step(index, carry):
        rows = pl.ds(pl.multiple_of(index * tile, tile), tile)
        value = jnp.dot(left[rows, :], right[...], preferred_element_type=jnp.float32)
        grad[rows, :] = value
        squared = value * value
        width = squared.shape[1]
        col_sums[...] += squared.reshape(tile // 8, 8, width).sum(axis=0)
        if lanes == 1:
            row_sums[rows, :] += squared.sum(axis=1, keepdims=True)
        else:
            groups = [squared[:, k : k + lanes] for k in range(0, width, lanes)]
            row_sums[rows, :] += sum(groups[1:], groups[0])
        return carry

    lax.fori_loop(0, left.shape[0] // tile, step, 0)


def gradient_columns(left, right, whole, start, width):
    rows, depth = left.shape
    size = right.shape[1]
    block = divisor_of((512, 256, 128), start, size) or size
    tile = divisor_of((384, 256, 128, 64, 32, 16, 8), rows)
    lanes = 128 if block % 128 == 0 else 1
    first = start // block
    held = () if whole is None else (whole,)
    return pl.pallas_call(
        functools.partial(gradient_kernel, tile),
        grid=(size // block,),
        in_specs=[
            pl.BlockSpec((rows, depth), lambda j: (0, 0)),
            pl.BlockSpec((depth, block), lambda j: (0, j)),
        ]
        + [pl.BlockSpec(memory_space=pl.ANY)] * len(held),
        out_specs=[
            pl.BlockSpec((rows, block), lambda j: (0, first + j)),
            pl.BlockSpec((8, block), lambda j: (0, j)),
            pl.BlockSpec((rows, lanes), lambda j: (0, 0)),
        ],
        out_shape=[
            jax.ShapeDtypeStruct((rows, width), jnp.float32),
            jax.ShapeDtypeStruct((8, size), jnp.float32),
            jax.ShapeDtypeStruct((rows, lanes), jnp.float32),
        ],
        input_output_aliases={2: 0} if held else {},
        compiler_params=pltpu.CompilerParams(
            dimension_semantics=("arbitrary",), vmem_limit_bytes=40 * 1024 * 1024
        ),
        cost_estimate=pl.CostEstimate(
            flops=2 * rows * depth * size,
            bytes_accessed=rows * size * 4 + depth * size * 2 + rows * depth * 2,
            transcendentals=0,
        ),
    )(left, right, *held)


def on_device(activations, output_grads, weight, row_moment, col_moment):
    tile_rows, tile_cols = weight.shape
    total_rows = tile_rows * lax.axis_size("row")
    total_cols = tile_cols * lax.axis_size("col")
    entries = float(total_rows * total_cols)
    cuts = column_cuts(tile_cols)
    grads = [lax.all_gather(output_grads[:, a:b], "row", axis=0, tiled=True) for a, b in cuts]
    left = gather_over(activations, "col").T
    weight_wide = weight.astype(jnp.float32)
    weight_local = jnp.sum(weight_wide * weight_wide)
    left, weight_local = lax.optimization_barrier((left, weight_local))
    gradient, row_part, col_parts = None, 0.0, [None] * len(cuts)
    for k in reversed(range(len(cuts))):
        gradient, col_sums, row_sums = gradient_columns(left, grads[k], gradient, cuts[k][0], tile_cols)
        row_part = row_part + row_sums
        col_parts[k] = jnp.sum(col_sums, axis=0)
    row_part = jnp.sum(row_part, axis=1)
    col_part = jnp.concatenate(col_parts)
    row_total = sum_over(row_part, "col") + total_cols * ADDED_SQUARE
    col_total = sum_over(col_part, "row") + total_rows * ADDED_SQUARE
    new_row = DECAY_RATE * row_moment + (1.0 - DECAY_RATE) * row_total / total_cols
    new_col = DECAY_RATE * col_moment + (1.0 - DECAY_RATE) * col_total / total_rows
    row_inverse = lax.rsqrt(new_row)
    col_inverse = lax.rsqrt(new_col)
    scaled = gradient * row_inverse[:, None] * col_inverse[None, :]
    ratio_local = jnp.sum(scaled * scaled)
    leader = (lax.axis_index("col") == 0).astype(jnp.float32)
    row_local = leader * jnp.sum(new_row)
    scalars = jnp.stack([row_local, weight_local, ratio_local])
    row_sum, weight_total, ratio_sum = sum_over(sum_over(scalars, "row"), "col")
    row_mean = row_sum / total_rows
    rms_update = jnp.sqrt(row_mean * ratio_sum / entries)
    clip_factor = jnp.maximum(1.0, rms_update / CLIP_LIMIT)
    step_scale = STEP_SIZE * jnp.sqrt(weight_total / entries + MEAN_OFFSET)
    row_factor = row_inverse * (step_scale / clip_factor * jnp.sqrt(row_mean))
    new_weight = (
        weight.astype(jnp.float32) - gradient * row_factor[:, None] * col_inverse[None, :]
    ).astype(jnp.bfloat16)
    return (new_weight, new_row, new_col)


def solution(mesh):
    return jax.shard_map(
        on_device,
        mesh=mesh,
        in_specs=(P("col", "row"), P("row", "col"), P("row", "col"), P("row"), P("col")),
        out_specs=(P("row", "col"), P("row"), P("col")),
        check_vma=False,
    )
```

time: 472 us -> 387 us (0.82)
  waiting for transfers between devices: 207 us -> 106 us
  blocking collectives: 81.3 us -> 0 us
  Pallas kernels: 0 us -> 73.4 us
  matrix products: 59.5 us -> 0 us
  local copies, waits for them, and re-layouts: 0.02 us -> 50.8 us
  starting transfers between devices: 0.08 us -> 18.1 us
  other arithmetic: 107 us -> 119 us
    all_gather x2 -> x4, waiting for transfers between devices: 205 us -> 45.5 us  [on_device(): lax.all_gather(output_grads[:, a:b], 'row', axis=0, tiled=True)]
    psum x3 -> x0, blocking collectives: 81.3 us -> none  [the longest x1 43.2 us: on_device(): row_sum, ratio_sum = lax.psum((row_local, ratio_local), ('row', 'col'))]
    pallas_call x0 -> x4, Pallas kernels: none -> 73.4 us  [gradient_columns(): pl.pallas_call(functools.partial(gradient_kernel, tile), grid=(size // bl...]
    ppermute x0 -> x17, waiting for transfers between devices: none -> 59.9 us  [swap(): return lax.ppermute(value, axis, [(i, i ^ stride) for i in range(size)])]
    dot_general x1 -> x0, matrix products: 59.5 us -> none  [on_device(): lax.dot_general(acts_all, lax.all_gather(output_grads, 'row', axis=0, til...]
    unnamed x8 -> x28, local copies, waits for them, and re-layouts: 0.02 us -> 21.2 us
    ppermute x0 -> x17, starting transfers between devices: none -> 17.9 us  [swap(): return lax.ppermute(value, axis, [(i, i ^ stride) for i in range(size)])]
    another operation x0 -> x2, local copies, waits for them, and re-layouts: none -> 13 us  [the longest x1 12.4 us: gather_over(): jnp.stack([jnp.where(upper, other, held), jnp.where(upper, held, other)],...]
  transfers between devices with their start and end apart: 2 -> 21, of which waited for: 2 -> 11; matrix products, arithmetic and copies ran while one was open for 5% -> 15% of each run, Pallas kernels for 0% -> 17%
where the time goes in v1:
time: 387 us; the launch traced here: 384 us
  other arithmetic  119 us (31%)
  waiting for transfers between devices  106 us (27%)
  Pallas kernels  73.4 us (19%)
  local copies, waits for them, and re-layouts  50.8 us (13%)
  starting transfers between devices  18.1 us (5%)
  between operations  16.6 us (4%)
    pallas_call x4, Pallas kernels, gradient_columns(): pl.pallas_call(functools.partial(gradient_kernel, tile), grid=(size // bl...  73.4 us
    ppermute x17, waiting for transfers between devices, swap(): return lax.ppermute(value, axis, [(i, i ^ stride) for i in range(size)])  59.9 us
    convert_element_type x1, other arithmetic, on_device(): new_weight = (weight.astype(jnp.float32) - gradient * row_factor[:, None]...  53.5 us
    all_gather x4, waiting for transfers between devices, on_device(): lax.all_gather(output_grads[:, a:b], 'row', axis=0, tiled=True)  45.5 us
    reduce_sum x1, other arithmetic, on_device(): ratio_local = jnp.sum(scaled * scaled)  27.9 us
    reduce_sum x1, other arithmetic, on_device(): weight_local = jnp.sum(weight_wide * weight_wide)  24.6 us
    unnamed x28, local copies, waits for them, and re-layouts  21.2 us
    ppermute x17, starting transfers between devices, swap(): return lax.ppermute(value, axis, [(i, i ^ stride) for i in range(size)])  17.9 us
  transfers between devices with their start and end apart: 21, of which 11 were waited for; matrix products, arithmetic and copies ran while one was open for 15% of the time, Pallas kernels for 17%

profile of v1, /device:TPU:12, one launch (start us, length us, event | category | flops | bytes accessed | tf_op | source)
XLA Modules:
  0.0 383.7 jit_solution(9625848477474062483)
XLA Ops:
  7.2 3.7 fusion.4
  11.0 0.7 all-gather.9.cloned.1.call-update
  11.8 2.3 slice.13
  14.1 2.7 collective-permute-start
  16.8 25.1 %collective-permute-done = bf16[128,2304]{1,0:T(8,128)(2,1)S(1)} collective-permute-done((bf16[128,2304]{1,0:T(8,128)(2,1)S(1)}, bf16[128,2304]{1,0:T(8,128)(2,1)S(1)}, u32[]{:S(2)}, u32[]{:S(2)}) %collective-permute-start) | collective-permute-done | bytes 589856 | tf_op jit(solution)/shard_map/ppermute | solution.py:20
  42.0 0.1 pad_maximum_fusion.2
  42.1 1.4 collective-permute-start.1
  43.5 1.9 slice.12
  45.5 24.6 %collective-permute-done.1 = bf16[2,128,2304]{2,1,0:T(8,128)(2,1)S(1)} collective-permute-done((bf16[2,128,2304]{2,1,0:T(8,128)(2,1)S(1)}, bf16[2,128,2304]{2,1,0:T(8,128)(2,1)S(1)}, u32[]{:S(2)}, u32[]{:S(2)}) %collective-permute-start.1) | collective-permute-done | bytes 1179680 | tf_op jit(solution)/shard_map/ppermute | solution.py:20
  70.1 0.2 select_bitcast_fusion.3
  70.2 0.2 pad_maximum_fusion.1
  70.5 24.6 %fusion = f32[]{:T(128)} fusion(bf16[2304,9216]{1,0:T(8,128)(2,1)} %param.7), kind=kLoop, calls=%fused_computation.2 | loop fusion | flops 63700992 | bytes 42467332 | tf_op jit(solution)/shard_map/reduce_sum | solution.py:148
  95.1 0.3 select_bitcast_fusion.1
  95.4 2.6 pad_maximum_fusion
  98.0 12.4 %copy.11 = bf16[2,2,2,128,2304]{3,2,1,0,4:T(2,128)(2,1)} copy(bf16[2,2,2,128,2304]{4,3,0,1,2:T(8,128)(2,1)} %pad_maximum_fusion) | data formatting | bytes 9437184 | tf_op jit(solution)/shard_map/stack | solution.py:50
  110.4 8.7 %reshape.26 = bf16[1024,2304]{0,1:T(8,128)(2,1)} reshape(bf16[2,2,2,128,2304]{3,2,1,0,4:T(2,128)(2,1)} %copy.11) | data formatting | bytes 9437184 | tf_op jit(solution)/shard_map/reshape | solution.py:53
  119.1 2.7 copy-done
  121.8 2.8 copy-done.11
  124.6 23.6 %shard_map.76 = (f32[2304,9216]{1,0:T(8,128)}, f32[8,3072]{1,0:T(8,128)S(1)}, f32[2304,128]{1,0:T(8,128)S(1)}) custom-call(bf16[2304,1024]{1,0:T(8,128)(2,1)S(1)} %bitcast.19, bf16[1024,3072]{1,0:T(8,128)(2,1)S(1)} %copy-done.11), custom_call_target="tpu_custom_call" | custom-call | flops 14495514624 | bytes 39321600 | tf_op jit(solution)/shard_map/pallas_call | solution.py:109
  148.3 0.6 copy-done.7
  148.9 5.3 %all-gather.9.cloned.1.call-done.right = bf16[1024,3072]{1,0:T(8,128)(2,1)} async-done(((bf16[256,3072]{1,0:T(8,128)(2,1)}), bf16[1024,3072]{1,0:T(8,128)(2,1)}) %all-gather.9.cloned.1.call-update) | async-done | bytes 6291472 | tf_op jit(solution)/shard_map/all_gather | solution.py:145
  154.2 2.3 copy-done.1
  156.5 2.8 copy-done.4
  159.3 23.7 %shard_map.77 = (f32[2304,9216]{1,0:T(8,128)}, f32[8,3072]{1,0:T(8,128)S(1)}, f32[2304,128]{1,0:T(8,128)S(1)}) custom-call(bf16[2304,1024]{1,0:T(8,128)(2,1)S(1)} %bitcast.20, bf16[1024,3072]{1,0:T(8,128)(2,1)S(1)} %copy-done.4, f32[2304,9216]{1,0:T(8,128)} %get-tuple-element.18.refs_0_), custom_call_target="tpu_custom_call", output_to_operand_aliasing={{0}: (2, {})} | custom-call | flops 14495514624 | bytes 39321600 | tf_op jit(solution)/shard_map/pallas_call | solution.py:109
  183.0 0.6 copy-done.8
  183.6 25.0 %all-gather.7.cloned.1.call-done.right = bf16[1024,2048]{1,0:T(8,128)(2,1)} async-done(((bf16[256,2048]{1,0:T(8,128)(2,1)}), bf16[1024,2048]{1,0:T(8,128)(2,1)}) %all-gather.7.cloned.1.call-update) | async-done | bytes 4194320 | tf_op jit(solution)/shard_map/all_gather | solution.py:145
  208.6 2.3 copy-done.2
  210.9 2.2 copy-done.5
  213.1 16.5 %shard_map.78 = (f32[2304,9216]{1,0:T(8,128)}, f32[8,2048]{1,0:T(8,128)S(1)}, f32[2304,128]{1,0:T(8,128)S(1)}) custom-call(bf16[2304,1024]{1,0:T(8,128)(2,1)S(1)} %bitcast.21, bf16[1024,2048]{1,0:T(8,128)(2,1)S(1)} %copy-done.5, f32[2304,9216]{1,0:T(8,128)} %get-tuple-element.19.refs_0_), custom_call_target="tpu_custom_call", output_to_operand_aliasing={{0}: (2, {})} | custom-call | flops 9663676416 | bytes 27787264 | tf_op jit(solution)/shard_map/pallas_call | solution.py:109
  229.7 0.6 copy-done.9
  230.3 15.2 %all-gather.5.cloned.1.call-done.right = bf16[1024,1024]{1,0:T(8,128)(2,1)} async-done(((bf16[256,1024]{1,0:T(8,128)(2,1)}), bf16[1024,1024]{1,0:T(8,128)(2,1)}) %all-gather.5.cloned.1.call-update) | async-done | bytes 2097168 | tf_op jit(solution)/shard_map/all_gather | solution.py:145
  245.5 2.3 copy-done.3
  247.9 1.6 copy-done.6
  249.4 9.5 %shard_map.79 = (f32[2304,9216]{1,0:T(8,128)}, f32[8,1024]{1,0:T(8,128)S(1)}, f32[2304,128]{1,0:T(8,128)S(1)}) custom-call(bf16[2304,1024]{1,0:T(8,128)(2,1)S(1)} %bitcast.22, bf16[1024,1024]{1,0:T(8,128)(2,1)S(1)} %copy-done.6, f32[2304,9216]{1,0:T(8,128)} %get-tuple-element.20.refs_0_), custom_call_target="tpu_custom_call", output_to_operand_aliasing={{0}: (2, {})} | custom-call | flops 4831838208 | bytes 16252928 | tf_op jit(solution)/shard_map/pallas_call | solution.py:109
  258.9 0.4 add_reduce_fusion
  259.3 0.2 copy-done.10
  259.6 0.5 collective-permute-start.4
  260.1 1.3 collective-permute-start.5
  261.4 0.8 reduce_sum.75
  262.2 0.9 reduce_sum.76
  263.1 0.9 reduce_sum.77
  264.0 0.9 reduce_sum.78
  265.0 2.5 collective-permute-start.6
  267.4 0.6 collective-permute-start.7
  268.0 1.5 collective-permute-start.8
  269.5 1.5 collective-permute-start.9
  270.9 1.3 fusion.2
  272.9 1.4 collective-permute-done.9
  274.3 1.4 fusion.3
  275.7 27.9 %multiply_reduce_fusion = f32[]{:T(128)} fusion(f32[2304,9216]{1,0:T(8,128)} %get-tuple-element.21, f32[9216]{0:T(1024)S(1)} %get-tuple-element.33, f32[2304]{0:T(1024)S(1)} %rsqrt.6), kind=kLoop, calls=%fused_computation.4 | loop fusion | flops 84934656 | bytes 84980736 | tf_op jit(solution)/shard_map/reduce_sum | solution.py:164
  303.6 1.4 pad_maximum_fusion.4
  305.0 0.6 collective-permute-start.10
  305.6 1.5 collective-permute-start.11
  307.0 1.5 collective-permute-start.12
  308.6 0.6 collective-permute-done.11
  309.1 2.4 collective-permute-done.12
  311.5 1.4 add_add_fusion.2
  312.9 0.6 collective-permute-start.14
  313.5 1.2 collective-permute-start.15
  314.7 1.8 collective-permute-done.14
  316.5 0.6 collective-permute-start.16
  317.1 4.0 %collective-permute-done.16 = f32[3]{0:T(128)S(1)} collective-permute-done((f32[3]{0:T(128)S(1)}, f32[3]{0:T(128)S(1)}, u32[]{:S(2)}, u32[]{:S(2)}) %collective-permute-start.16) | collective-permute-done | bytes 44 | tf_op jit(solution)/shard_map/ppermute | solution.py:20
  321.0 0.6 fusion.5
  323.7 53.5 %fusion.1 = bf16[2304,9216]{1,0:T(8,128)(2,1)} fusion(bf16[2304,9216]{1,0:T(8,128)(2,1)} %param.7, f32[2304,9216]{1,0:T(8,128)} %get-tuple-element.21, f32[2304]{0:T(1024)S(1)} %broadcast_multiply_fusion, f32[9216]{0:T(1024)S(1)} %get-tuple-element.33), kind=kLoop, calls=%fused_computation.3 | loop fusion | flops 106168320 | bytes 169915392 | tf_op jit(solution)/shard_map/convert_element_type | solution.py:176
  (44 shorter events, 0.5 us)
Async XLA Ops:
  7.2 112.0 %all-gather.11.cloned.1.call-start = ((), (), s32[]{:S(2)}) async-start(), calls=%async_computation.3 | async-start | bytes 7864320 | tf_op jit(solution)/shard_map/all_gather | solution.py:145
  11.0 143.2 %all-gather.9.cloned.1.call-start = ((), (), s32[]{:S(2)}) async-start(), calls=%async_computation.2 | async-start | bytes 7864320 | tf_op jit(solution)/shard_map/all_gather | solution.py:145
  11.0 3.1 copy-start.12
  11.7 196.9 %all-gather.7.cloned.1.call-start = ((), (), s32[]{:S(2)}) async-start(), calls=%async_computation.1 | async-start | bytes 5242880 | tf_op jit(solution)/shard_map/all_gather | solution.py:145
  14.1 231.4 %all-gather.5.cloned.1.call-start = ((), (), s32[]{:S(2)}) async-start(), calls=%async_computation | async-start | bytes 2621440 | tf_op jit(solution)/shard_map/all_gather | solution.py:145
  14.1 27.8 %collective-permute-start = (bf16[128,2304]{1,0:T(8,128)(2,1)S(1)}, bf16[128,2304]{1,0:T(8,128)(2,1)S(1)}, u32[]{:S(2)}, u32[]{:S(2)}) collective-permute-start(bf16[128,2304]{1,0:T(8,128)(2,1)S(1)} %copy-done.12), channel_id=1, source_target_pairs={{0,4},{1,5},{2,6},{3,7},{4,0},{5,1},{6,2},{7,3},{8,12},{9,13},{10,... | collective-permute-start | bytes 1769480 | tf_op jit(solution)/shard_map/ppermute | solution.py:20
  42.1 28.0 %collective-permute-start.1 = (bf16[2,128,2304]{2,1,0:T(8,128)(2,1)S(1)}, bf16[2,128,2304]{2,1,0:T(8,128)(2,1)S(1)}, u32[]{:S(2)}, u32[]{:S(2)}) collective-permute-start(bf16[2,128,2304]{2,1,0:T(8,128)(2,1)S(1)} %pad_maximum_fusion.2), channel_id=1, source_target_pairs={{0,2},{1,3},{2,0},{3,1},{4,6},{5,7},{6,4},{7,5},{8,10},{9,11},{10,... | collective-permute-start | bytes 3538952 | tf_op jit(solution)/shard_map/ppermute | solution.py:20
  70.5 24.7 %collective-permute-start.2 = (bf16[2,2,128,2304]{3,2,0,1:T(8,128)(2,1)S(1)}, bf16[2,2,128,2304]{3,2,0,1:T(8,128)(2,1)S(1)}, u32[]{:S(2)}, u32[]{:S(2)}) collective-permute-start(bf16[2,2,128,2304]{3,2,0,1:T(8,128)(2,1)S(1)} %pad_maximum_fusion.1), channel_id=1, source_target_pairs={{0,1},{1,0},{2,3},{3,2},{4,5},{5,4},{6,7},{7,6},{8,9},{9,8},{10,11... | collective-permute-start | bytes 7077896 | tf_op jit(solution)/shard_map/ppermute | solution.py:20
  119.1 2.7 copy-start
  121.8 2.8 copy-start.11
  148.2 0.6 copy-start.7
  154.2 2.3 copy-start.1
  156.5 2.8 copy-start.4
  183.0 0.6 copy-start.8
  208.6 2.3 copy-start.2
  210.9 2.2 copy-start.5
  229.7 0.6 copy-start.9
  245.5 2.3 copy-start.3
  247.9 1.6 copy-start.6
  258.9 0.6 copy-start.10
  259.6 5.4 %collective-permute-start.3 = (f32[2304]{0:T(1024)S(1)}, f32[2304]{0:T(1024)S(1)}, u32[]{:S(2)}, u32[]{:S(2)}) collective-permute-start(f32[2304]{0:T(1024)S(1)} %add_reduce_fusion), channel_id=1, source_target_pairs={{0,1},{1,0},{2,3},{3,2},{4,5},{5,4},{6,7},{7,6},{8,9},{9,8},{10,11... | collective-permute-start | bytes 27656 | tf_op jit(solution)/shard_map/ppermute | solution.py:20
  259.6 5.4 %collective-permute-start.4 = (f32[2304]{0:T(1024)S(1)}, f32[2304]{0:T(1024)S(1)}, u32[]{:S(2)}, u32[]{:S(2)}) collective-permute-start(f32[2304]{0:T(1024)S(1)} %add_reduce_fusion), channel_id=1, source_target_pairs={{0,2},{1,3},{2,0},{3,1},{4,6},{5,7},{6,4},{7,5},{8,10},{9,11},{10,... | collective-permute-start | bytes 27656 | tf_op jit(solution)/shard_map/ppermute | solution.py:20
  260.1 4.8 %collective-permute-start.5 = (f32[2304]{0:T(1024)S(1)}, f32[2304]{0:T(1024)S(1)}, u32[]{:S(2)}, u32[]{:S(2)}) collective-permute-start(f32[2304]{0:T(1024)S(1)} %add_reduce_fusion), channel_id=1, source_target_pairs={{0,3},{1,2},{2,1},{3,0},{4,7},{5,6},{6,5},{7,4},{8,11},{9,10},{10,... | collective-permute-start | bytes 27656 | tf_op jit(solution)/shard_map/ppermute | solution.py:20
  265.0 6.0 %collective-permute-start.6 = (f32[2304]{0:T(1024)S(1)}, f32[2304]{0:T(1024)S(1)}, u32[]{:S(2)}, u32[]{:S(2)}) collective-permute-start(f32[2304]{0:T(1024)S(1)} %add_add_fusion), channel_id=1, source_target_pairs={{0,4},{1,5},{2,6},{3,7},{4,0},{5,1},{6,2},{7,3},{8,12},{9,13},{10,... | collective-permute-start | bytes 27656 | tf_op jit(solution)/shard_map/ppermute | solution.py:20
  267.4 5.5 %collective-permute-start.7 = (f32[9216]{0:T(1024)S(1)}, f32[9216]{0:T(1024)S(1)}, u32[]{:S(2)}, u32[]{:S(2)}) collective-permute-start(f32[9216]{0:T(1024)S(1)} %pad_maximum_fusion.3), channel_id=1, source_target_pairs={{0,8},{8,0},{16,24},{24,16},{1,9},{9,1},{17,25},{25,17},{2,10},{10... | collective-permute-start | bytes 110600 | tf_op jit(solution)/shard_map/ppermute | solution.py:20
  268.0 4.9 %collective-permute-start.8 = (f32[9216]{0:T(1024)S(1)}, f32[9216]{0:T(1024)S(1)}, u32[]{:S(2)}, u32[]{:S(2)}) collective-permute-start(f32[9216]{0:T(1024)S(1)} %pad_maximum_fusion.3), channel_id=1, source_target_pairs={{0,16},{8,24},{16,0},{24,8},{1,17},{9,25},{17,1},{25,9},{2,18},{10... | collective-permute-start | bytes 110600 | tf_op jit(solution)/shard_map/ppermute | solution.py:20
  269.5 4.9 %collective-permute-start.9 = (f32[9216]{0:T(1024)S(1)}, f32[9216]{0:T(1024)S(1)}, u32[]{:S(2)}, u32[]{:S(2)}) collective-permute-start(f32[9216]{0:T(1024)S(1)} %pad_maximum_fusion.3), channel_id=1, source_target_pairs={{0,24},{8,16},{16,8},{24,0},{1,25},{9,17},{17,9},{25,1},{2,26},{10... | collective-permute-start | bytes 110600 | tf_op jit(solution)/shard_map/ppermute | solution.py:20
  272.2 51.4 %copy-start.13 = (f32[2304]{0:T(1024)}, f32[2304]{0:T(1024)S(1)}, u32[]{:S(2)}) copy-start(f32[2304]{0:T(1024)S(1)} %get-tuple-element.32) | copy-start | bytes 27652
  305.0 3.6 collective-permute-start.10
  305.6 3.6 collective-permute-start.11
  307.0 4.5 %collective-permute-start.12 = (f32[3]{0:T(128)S(1)}, f32[3]{0:T(128)S(1)}, u32[]{:S(2)}, u32[]{:S(2)}) collective-permute-start(f32[3]{0:T(128)S(1)} %pad_maximum_fusion.4), channel_id=1, source_target_pairs={{0,24},{8,16},{16,8},{24,0},{1,25},{9,17},{17,9},{25,1},{2,26},{10... | collective-permute-start | bytes 44 | tf_op jit(solution)/shard_map/ppermute | solution.py:20
  312.8 1.9 collective-permute-start.13
  312.9 3.6 collective-permute-start.14
  313.5 3.0 collective-permute-start.15
  316.5 4.5 %collective-permute-start.16 = (f32[3]{0:T(128)S(1)}, f32[3]{0:T(128)S(1)}, u32[]{:S(2)}, u32[]{:S(2)}) collective-permute-start(f32[3]{0:T(128)S(1)} %add_add_fusion.1), channel_id=1, source_target_pairs={{0,4},{1,5},{2,6},{3,7},{4,0},{5,1},{6,2},{7,3},{8,12},{9,13},{10,... | collective-permute-start | bytes 44 | tf_op jit(solution)/shard_map/ppermute | solution.py:20
Sparse Core Ops, SparseCore 0:
  11.1 71.1 all-gather.10
  84.1 70.0 all-gather.8
  156.0 52.5 all-gather.6
  210.3 35.1 all-gather.4
